TPU v7x, 128 devices: a whole 4x4x4 slice. The times are simulated.
128 devices in a mesh: rows: 4 (over y_lo, core), cols: 32 (over z, x, y_hi).
Axes of the slice: x: 4, y: 4 (y_hi: 2, y_lo: 2; y = y_hi * 2 + y_lo), z: 4, core: 2. Of those that a mesh axis runs over, the one named last changes fastest.
Arguments:
- object_field: float32 [2, 512, 4096], P(None, 'rows', 'cols'), may hold values from -6 to 6
- probe: float32 [2, 256, 256], replicated, may hold values from -6 to 6
- amplitudes: float32 [4, 32, 4, 256, 256], P('rows', 'cols'), may hold values from 0.5 to 4
- offsets: int32 [4, 32, 4, 2], P('rows', 'cols'), may hold values from 0 to 128
Outputs:
- updated: float32 [2, 512, 4096], P(None, 'rows', 'cols')
Inputs may be any that keep to these rules, and one draw needn't show every extreme that they name: `offsets`: every window lies inside its tile's extended region of 384 cells a side.
All inputs are finite; a program needn't handle non-finite values.
Results may differ from a plain program's by a relative error of at most 0.0001.
Values sent between devices are 32-bit elements; how exact they have to be, the bound alone decides.
A program may use at most 64 MiB of HBM per device.

v0:
```python
import functools
import math

import jax
import jax.numpy as jnp
import numpy as np
from jax import lax
from jax.experimental import pallas as pl
from jax.experimental.pallas import tpu as pltpu
from jax.sharding import PartitionSpec as P

ITERS = 2
T = 128
W = 256
MESH = pl.DeviceIdType.MESH
f32 = jnp.float32
bf16 = jnp.bfloat16


def dft_parts():
    m = np.arange(T)
    mats = []
    for odd in (0, 1):
        turns = (m[:, None] * (2 * m[None, :] + odd)) % W
        angle = 2.0 * np.pi / W * turns
        c, s = np.cos(angle) / 16.0, np.sin(angle) / 16.0
        mats.append(np.block([[c, -s], [s, c]]))
    mats = [mats[0], mats[1], mats[0].T, mats[1].T]
    out = []
    for a in mats:
        a = a.astype(np.float32)
        hi = a.astype(jnp.bfloat16)
        lo = (a - hi.astype(np.float32)).astype(jnp.bfloat16)
        out += [hi, lo]
    return np.stack(out)


def split(x):
    hi = x.astype(bf16)
    return hi, (x - hi.astype(f32)).astype(bf16)


def mm(a, b):
    return jnp.dot(a, b, preferred_element_type=f32)


def kernel(
    n_rows, n_cols, n_pos,
    obj_ref, off_ref, probe_hbm, amp_hbm, mats_hbm,
    out_ref,
    G, A, FC, FX, FY, ill, probe, amp, mats, rolled, ampp, halves,
    g_send, g_recv, f_send, f_recv, l_sem,
):
    r = lax.axis_index("rows")
    c = lax.axis_index("cols")
    ro, h = lax.rem(r, 2), lax.rem(c, 2)
    rc, rx = r + 1 - 2 * ro, r - 1 + 2 * ro
    cp = c + 1 - 2 * h
    cx, cf = c + 2 - 4 * h, c - 2 + 4 * h
    has_x = (rx >= 0) & (rx < n_rows)
    has_cx = (cx >= 0) & (cx < n_cols)
    has_far = (cf >= 0) & (cf < n_cols)
    rcs = rc - r + 1
    rxs = 2 - rcs
    hp = cp - c + 1
    fp = 2 - hp

    local = [
        pltpu.make_async_copy(probe_hbm, probe, l_sem.at[0]),
        pltpu.make_async_copy(amp_hbm, amp, l_sem.at[1]),
        pltpu.make_async_copy(mats_hbm, mats, l_sem.at[2]),
    ]
    for copy in local:
        copy.start()

    barrier = pltpu.get_barrier_semaphore()

    def greet(row, col):
        pl.semaphore_signal(
            barrier, inc=1, device_id={"rows": row, "cols": col}, device_id_type=MESH
        )

    greet(rc, c)
    greet(r, cp)

    @pl.when(has_x)
    def _():
        greet(rx, c)
        greet(rx, cp)

    @pl.when(has_cx)
    def _():
        greet(r, cx)

    @pl.when(has_far)
    def _():
        greet(r, cf)

    always = None

    def both(a, b):
        return a & b

    def when(cond, f):
        if cond is None:
            f()
        else:
            pl.when(cond)(f)

    g_sends = {2: has_x, 3: has_x, 4: has_cx, 5: both(has_x, has_cx), 7: has_far}
    g_recvs = {2: has_x, 3: has_x, 4: has_far, 5: both(has_x, has_far), 7: has_far}

    def g_copy(L, k):
        src, dst, dev = {
            0: ((1, 1), (2 - rcs, 1), (rc, c)),
            1: ((1, 1), (1, 2 - hp), (r, cp)),
            2: ((1, 1), (2 - rxs, 1), (rx, c)),
            3: ((1, 1), (2 - rxs, 2 - hp), (rx, cp)),
            4: ((1, hp), (1, fp), (r, cx)),
            5: ((rxs, hp), (rxs, fp), (r, cx)),
            6: ((1, hp), (2 - rcs, hp), (rc, c)),
            7: ((1, fp), (2 - rcs, fp), (rc, c)),
        }[k]
        return pltpu.make_async_remote_copy(
            src_ref=G.at[(L,) + src],
            dst_ref=G.at[(L,) + dst],
            send_sem=g_send.at[L, k],
            recv_sem=g_recv.at[L, k],
            device_id={"rows": dev[0], "cols": dev[1]},
            device_id_type=MESH,
        )

    def g_start(L, k):
        when(g_sends.get(k, always), lambda: g_copy(L, k).start())

    def g_wait(L, k):
        when(g_recvs.get(k, always), lambda: g_copy(L, k).wait_recv())

    def g_begin(planes):
        for L in planes:
            for k in (1, 3, 2, 0):
                g_start(L, k)

    def g_finish(planes):
        for L in planes:
            g_wait(L, 1)
            g_start(L, 4)
            g_start(L, 6)
            g_wait(L, 3)
            g_start(L, 5)
        for L in planes:
            g_wait(L, 4)
            g_start(L, 7)
        for L in planes:
            for k in (0, 2, 5, 6, 7):
                g_wait(L, k)

    f_sends = {1: has_far, 2: both(has_x, has_far), 4: has_x, 5: has_x}
    f_recvs = {1: has_cx, 2: both(has_x, has_cx), 4: has_x, 5: has_x}

    def f_copy(L, k):
        src, dst, dev = {
            0: (A.at[L, rcs], FC.at[L], (rc, c)),
            1: (A.at[L, 1, fp], FX.at[L, 0], (r, cf)),
            2: (A.at[L, rxs, fp], FX.at[L, 1], (r, cf)),
            3: (A.at[L, 1, hp], FY.at[L, 0], (r, cp)),
            4: (A.at[L, rxs, 1], FY.at[L, 1], (rx, c)),
            5: (A.at[L, rxs, hp], FY.at[L, 2], (rx, cp)),
        }[k]
        return pltpu.make_async_remote_copy(
            src_ref=src,
            dst_ref=dst,
            send_sem=f_send.at[L, k],
            recv_sem=f_recv.at[L, k],
            device_id={"rows": dev[0], "cols": dev[1]},
            device_id_type=MESH,
        )

    def f_start(L, k):
        when(f_sends.get(k, always), lambda: f_copy(L, k).start())

    def f_wait(L, k):
        when(f_recvs.get(k, always), lambda: f_copy(L, k).wait_recv())

    def f_begin(planes):
        for L in planes:
            for k in (0, 2, 4):
                f_start(L, k)

    def f_core(planes):
        for L in planes:
            f_wait(L, 0)
            A[L, 1, fp] += FC[L, fp]
            f_start(L, 1)
        for L in planes:
            A[L, 1, hp] += FC[L, hp]

    def f_across(planes):
        for L in planes:
            f_wait(L, 2)

            @pl.when(f_recvs[2])
            def _():
                A[L, rxs, hp] += FX[L, 1]

            f_start(L, 5)
            f_wait(L, 1)

            @pl.when(has_cx)
            def _():
                A[L, 1, hp] += FX[L, 0]

            f_start(L, 3)

    def f_end(L):
        f_wait(L, 3)
        f_wait(L, 4)
        f_wait(L, 5)
        return A[L, 1, 1] + FC[L, 1] + FY[L, 0] + FY[L, 1] + FY[L, 2]

    for plane in range(2):
        G[plane, 1, 1] = obj_ref[plane]
    greeted = 2 + 2 * has_x.astype(jnp.int32) + has_cx.astype(jnp.int32) + has_far.astype(jnp.int32)
    pl.semaphore_wait(barrier, greeted)
    g_begin((0, 1))

    zero_tile = jnp.zeros((T, T), f32)

    @pl.when(jnp.logical_not(has_x))
    def _():
        for L in range(2 * ITERS):
            for col in range(3):
                G[L, rxs, col] = zero_tile
        for L in range(2 * ITERS + 1):
            FY[L, 1] = zero_tile
            FY[L, 2] = zero_tile

    @pl.when(jnp.logical_not(has_far))
    def _():
        for L in range(2 * ITERS):
            for row in range(3):
                G[L, row, fp] = zero_tile

    for L in range(2 * ITERS + 1):
        for row in range(3):
            for col in range(3):
                A[L, row, col] = zero_tile

    row_of = lax.broadcasted_iota(jnp.int32, (T, T), 0)
    col_of = lax.broadcasted_iota(jnp.int32, (T, T), 1)

    def add_term(L, p, term):
        mr = row_of >= off_ref[p, 0]
        mc = col_of >= off_ref[p, 1]
        zero = jnp.zeros((T, T), f32)
        top = jnp.where(mr, term[0][0], zero)
        low = term[0][0] - top
        A[L, 0, 0] += jnp.where(mc, top, zero)
        A[L, 0, 2] += jnp.where(mc, zero, top)
        A[L, 2, 0] += jnp.where(mc, low, zero)
        A[L, 2, 2] += jnp.where(mc, zero, low)
        A[L, 0, 1] += jnp.where(mr, term[0][1], zero)
        A[L, 2, 1] += jnp.where(mr, zero, term[0][1])
        A[L, 1, 0] += jnp.where(mc, term[1][0], zero)
        A[L, 1, 2] += jnp.where(mc, zero, term[1][0])
        A[L, 1, 1] += term[1][1]

    def blocks(x):
        return [[x[i * T:(i + 1) * T, j * T:(j + 1) * T] for j in range(2)] for i in range(2)]

    local[0].wait()

    def roll_probe(p, carry):
        power = None
        for plane in range(2):
            x = pltpu.roll(probe[plane], off_ref[p, 0], 0)
            x = pltpu.roll(x, off_ref[p, 1], 1)
            rolled[p, plane] = x
            power = x * x if power is None else power + x * x
        add_term(2 * ITERS, p, blocks(power))
        return carry

    lax.fori_loop(0, n_pos, roll_probe, 0)

    local[1].wait()
    lane_in = lax.broadcasted_iota(jnp.int32, (W, W), 0)
    lane_out = lax.broadcasted_iota(jnp.int32, (W, W), 1)
    source = jnp.where(lane_out < T, 2 * lane_out, 2 * lane_out - (W - 1))
    perm = jnp.where(lane_in == source, 1.0, 0.0).astype(bf16)

    def permute_amp(p, carry):
        x = amp[p]
        hi = x.astype(bf16)
        mid, low = split(x - hi.astype(f32))
        x = mm(hi, perm) + mm(mid, perm) + mm(low, perm)
        for half in range(2):
            lanes = pl.ds(half * T, T)
            halves[half] = x[:, half * T:(half + 1) * T]
            for par in range(2):
                ampp[p, par, :, lanes] = halves[half, pl.ds(par, T, stride=2), :]
        return carry

    lax.fori_loop(0, n_pos, permute_amp, 0)
    local[2].wait()

    def right(x, m):
        hi, lo = split(x)
        return mm(hi, mats[m]) + mm(lo, mats[m]) + mm(hi, mats[m + 1])

    def left(m, x):
        hi, lo = split(x)
        return mm(mats[m], hi) + mm(mats[m + 1], hi) + mm(mats[m], lo)

    def window(it, p):
        mr = row_of >= off_ref[p, 0]
        mc = col_of >= off_ref[p, 1]
        ob = []
        for L in (2 * it, 2 * it + 1):
            t = lambda a, b: G[L, a, b]
            ob.append([
                [
                    jnp.where(mr, jnp.where(mc, t(0, 0), t(0, 2)), jnp.where(mc, t(2, 0), t(2, 2))),
                    jnp.where(mr, t(0, 1), t(2, 1)),
                ],
                [jnp.where(mc, t(1, 0), t(1, 2)), t(1, 1)],
            ])
        pr = blocks(rolled[p, 0])
        pi = blocks(rolled[p, 1])
        us, vs = [], []
        for i in range(2):
            er = [pr[i][j] * ob[0][i][j] - pi[i][j] * ob[1][i][j] for j in range(2)]
            ei = [pr[i][j] * ob[1][i][j] + pi[i][j] * ob[0][i][j] for j in range(2)]
            us.append(jnp.concatenate([er[0] + er[1], ei[0] + ei[1]], 1))
            vs.append(jnp.concatenate([er[0] - er[1], ei[0] - ei[1]], 1))
        even = right(jnp.concatenate(us, 0), 0)
        odd = right(jnp.concatenate(vs, 0), 2)
        yr = jnp.concatenate([even[:, :T], odd[:, :T]], 1)
        yi = jnp.concatenate([even[:, T:], odd[:, T:]], 1)
        u = jnp.concatenate([yr[:T] + yr[T:], yi[:T] + yi[T:]], 0)
        v = jnp.concatenate([yr[:T] - yr[T:], yi[:T] - yi[T:]], 0)
        back = []
        for par, x in ((0, u), (1, v)):
            far = left(4 + 2 * par, x)
            fr, fi = far[:T], far[T:]
            keep = 1.0 - ampp[p, par] * lax.rsqrt(jnp.maximum(fr * fr + fi * fi, 0.25))
            back.append(left(2 * par, jnp.concatenate([fr * keep, fi * keep], 0)))
        tot, dif = back[0] + back[1], back[0] - back[1]
        zr = jnp.concatenate([tot[:T], dif[:T]], 0)
        zi = jnp.concatenate([tot[T:], dif[T:]], 0)
        even = right(jnp.concatenate([zr[:, :T], zi[:, :T]], 1), 4)
        odd = right(jnp.concatenate([zr[:, T:], zi[:, T:]], 1), 6)
        tot, dif = even + odd, even - odd
        tr, ti = [], []
        for i in range(2):
            rows = slice(i * T, (i + 1) * T)
            br = [tot[rows, :T], dif[rows, :T]]
            bi = [tot[rows, T:], dif[rows, T:]]
            tr.append([pr[i][j] * br[j] + pi[i][j] * bi[j] for j in range(2)])
            ti.append([pr[i][j] * bi[j] - pi[i][j] * br[j] for j in range(2)])
        add_term(2 * it, p, tr)
        add_term(2 * it + 1, p, ti)

    def windows(it, first, last):
        def step(p, carry):
            window(it, p)
            return carry

        lax.fori_loop(first, last, step, 0)

    g_finish((0, 1))
    light = (2 * ITERS,)
    f_begin(light)
    for it in range(ITERS):
        if it == 0:
            half = n_pos // 2
            windows(it, 0, half)
            f_core(light)
            windows(it, half, n_pos)
        else:
            windows(it, 0, n_pos)
        planes = (2 * it, 2 * it + 1)
        f_begin(planes)
        if it == 0:
            f_across(light)
        f_core(planes)
        f_across(planes)
        if it == 0:
            ill[...] = f_end(2 * ITERS) + 1.0
        for plane in range(2):
            L = 2 * it + plane
            new = G[L, 1, 1] - f_end(L) / ill[...]
            if it < ITERS - 1:
                G[L + 2, 1, 1] = new
                g_begin((L + 2,))
            else:
                out_ref[plane] = new
        if it < ITERS - 1:
            g_finish((2 * it + 2, 2 * it + 3))

    for L in range(2 * ITERS):
        for k in range(8):
            when(g_sends.get(k, always), lambda L=L, k=k: g_copy(L, k).wait_send())
    for L in range(2 * ITERS + 1):
        for k in range(6):
            when(f_sends.get(k, always), lambda L=L, k=k: f_copy(L, k).wait_send())


def local(n_rows, n_cols, object_field, probe, amplitudes, offsets):
    n_pos = amplitudes.shape[2]
    n = 2 * ITERS
    anyspace = pl.BlockSpec(memory_space=pl.ANY)
    vmem = pl.BlockSpec(memory_space=pltpu.VMEM)
    return pl.pallas_call(
        functools.partial(kernel, n_rows, n_cols, n_pos),
        out_shape=jax.ShapeDtypeStruct(object_field.shape, f32),
        in_specs=[vmem, pl.BlockSpec(memory_space=pltpu.SMEM), anyspace, anyspace, anyspace],
        out_specs=vmem,
        scratch_shapes=[
            pltpu.VMEM((n, 3, 3, T, T), f32),
            pltpu.VMEM((n + 1, 3, 3, T, T), f32),
            pltpu.VMEM((n + 1, 3, T, T), f32),
            pltpu.VMEM((n + 1, 2, T, T), f32),
            pltpu.VMEM((n + 1, 3, T, T), f32),
            pltpu.VMEM((T, T), f32),
            pltpu.VMEM((2, W, W), f32),
            pltpu.VMEM((n_pos, W, W), f32),
            pltpu.VMEM((8, W, W), bf16),
            pltpu.VMEM((n_pos, 2, W, W), f32),
            pltpu.VMEM((n_pos, 2, T, W), f32),
            pltpu.VMEM((2, W, T), f32),
            pltpu.SemaphoreType.DMA((n, 8)),
            pltpu.SemaphoreType.DMA((n, 8)),
            pltpu.SemaphoreType.DMA((n + 1, 6)),
            pltpu.SemaphoreType.DMA((n + 1, 6)),
            pltpu.SemaphoreType.DMA((3,)),
        ],
        compiler_params=pltpu.CompilerParams(
            collective_id=0, has_side_effects=True, vmem_limit_bytes=56 * 1024 * 1024
        ),
    )(
        object_field,
        offsets[0, 0],
        probe,
        amplitudes[0, 0],
        jnp.asarray(dft_parts()),
    )


def solution(mesh):
    placed = (
        P(None, "rows", "cols"),
        P(),
        P("rows", "cols", None, None, None),
        P("rows", "cols", None, None),
    )
    body = functools.partial(local, mesh.shape["rows"], mesh.shape["cols"])
    return jax.shard_map(
        body, mesh=mesh, in_specs=placed, out_specs=P(None, "rows", "cols"), check_vma=False
    )
```

profile of v0, /device:TPU:96, one launch (start us, length us, event | category | flops | bytes accessed | tf_op | source)
XLA Modules:
  0.0 69.9 jit_solution(4423654690117289176)
XLA Ops:
  0.0 0.0 copy-start
  0.0 0.7 copy-done
  0.7 0.7 copy.6.off_ref
  1.3 67.0 %shard_map.55 = f32[2,128,128]{2,1,0:T(8,128)} custom-call(f32[2,128,128]{2,1,0:T(8,128)} %obj_ref.1, s32[4,2]{1,0:T(4,128)} %copy.6.off_ref, f32[2,256,256]{2,1,0:T(8,128)} %probe_hbm.1, f32[4,256,256]{2,1,0:T(8,128)} %bitcast.2, bf16[8,256,256]{2,1,0:T(8,128)(2,1)} %constant.2.clone.mats_hbm), custom_call_target="tpu_custom_call" | custom-call | tf_op jit(solution)/shard_map/pallas_call | solution.py:413
  68.3 1.6 %copy.8 = f32[2,128,128]{2,1,0:T(8,128)} copy(f32[2,128,128]{2,1,0:T(8,128)} %shard_map.55) | data formatting | bytes 262144
Async XLA Ops:
  0.0 0.7 copy-start
where the time goes:
time: 70.5 us; the launch traced here: 69.9 us
  Pallas kernels  67 us (95%)
  local copies, waits for them, and re-layouts  2.91 us (4%)
    pallas_call x1, Pallas kernels, local(): pl.pallas_call(functools.partial(kernel, n_rows, n_cols, n_pos), out_shap...  67 us
    unnamed x3, local copies, waits for them, and re-layouts  2.25 us

commit v1 on v0

--- a/solution.py
+++ b/solution.py
@@ -12,6 +12,9 @@
 ITERS = 2
 T = 128
 W = 256
+CHUNK = 64
+GROUP = 2
+VMEM_MIB = 28
 MESH = pl.DeviceIdType.MESH
 f32 = jnp.float32
 bf16 = jnp.bfloat16
@@ -46,7 +49,7 @@
 
 def kernel(
     n_rows, n_cols, n_pos,
-    obj_ref, off_ref, probe_hbm, amp_hbm, mats_hbm,
+    obj_hbm, off_ref, probe_hbm, amp_hbm, mats_hbm,
     out_ref,
     G, A, FC, FX, FY, ill, probe, amp, mats, rolled, ampp, halves,
     g_send, g_recv, f_send, f_recv, l_sem,
@@ -69,9 +72,11 @@
         pltpu.make_async_copy(probe_hbm, probe, l_sem.at[0]),
         pltpu.make_async_copy(amp_hbm, amp, l_sem.at[1]),
         pltpu.make_async_copy(mats_hbm, mats, l_sem.at[2]),
+        pltpu.make_async_copy(obj_hbm.at[0], G.at[0, 1, 1], l_sem.at[3]),
+        pltpu.make_async_copy(obj_hbm.at[1], G.at[1, 1, 1], l_sem.at[4]),
     ]
-    for copy in local:
-        copy.start()
+    for i in (3, 4, 0, 1, 2):
+        local[i].start()
 
     barrier = pltpu.get_barrier_semaphore()
 
@@ -110,7 +115,7 @@
     g_sends = {2: has_x, 3: has_x, 4: has_cx, 5: both(has_x, has_cx), 7: has_far}
     g_recvs = {2: has_x, 3: has_x, 4: has_far, 5: both(has_x, has_far), 7: has_far}
 
-    def g_copy(L, k):
+    def g_copy(L, k, q):
         src, dst, dev = {
             0: ((1, 1), (2 - rcs, 1), (rc, c)),
             1: ((1, 1), (1, 2 - hp), (r, cp)),
@@ -121,108 +126,123 @@
             6: ((1, hp), (2 - rcs, hp), (rc, c)),
             7: ((1, fp), (2 - rcs, fp), (rc, c)),
         }[k]
+        part = (pl.ds(q * CHUNK, CHUNK),)
         return pltpu.make_async_remote_copy(
-            src_ref=G.at[(L,) + src],
-            dst_ref=G.at[(L,) + dst],
-            send_sem=g_send.at[L, k],
-            recv_sem=g_recv.at[L, k],
+            src_ref=G.at[(L,) + src + part],
+            dst_ref=G.at[(L,) + dst + part],
+            send_sem=g_send.at[L, k, q],
+            recv_sem=g_recv.at[L, k, q],
             device_id={"rows": dev[0], "cols": dev[1]},
             device_id_type=MESH,
         )
 
-    def g_start(L, k):
-        when(g_sends.get(k, always), lambda: g_copy(L, k).start())
-
-    def g_wait(L, k):
-        when(g_recvs.get(k, always), lambda: g_copy(L, k).wait_recv())
-
-    def g_begin(planes):
-        for L in planes:
-            for k in (1, 3, 2, 0):
-                g_start(L, k)
+    def g_start(L, k, q):
+        when(g_sends.get(k, always), lambda: g_copy(L, k, q).start())
+
+    def g_wait(L, k, q):
+        when(g_recvs.get(k, always), lambda: g_copy(L, k, q).wait_recv())
+
+    def chunks(planes):
+        return [(L, q) for L in planes for q in range(T // CHUNK)]
+
+    def g_begin(planes, kinds):
+        for k in kinds:
+            for L, q in chunks(planes):
+                g_start(L, k, q)
 
     def g_finish(planes):
-        for L in planes:
-            g_wait(L, 1)
-            g_start(L, 4)
-            g_start(L, 6)
-            g_wait(L, 3)
-            g_start(L, 5)
-        for L in planes:
-            g_wait(L, 4)
-            g_start(L, 7)
-        for L in planes:
-            for k in (0, 2, 5, 6, 7):
-                g_wait(L, k)
+        for L, q in chunks(planes):
+            g_wait(L, 1, q)
+            g_start(L, 4, q)
+            g_start(L, 6, q)
+        for L, q in chunks(planes):
+            g_wait(L, 3, q)
+            g_start(L, 5, q)
+        for L, q in chunks(planes):
+            g_wait(L, 4, q)
+            g_start(L, 7, q)
+        for k in (0, 2, 5, 6, 7):
+            for L, q in chunks(planes):
+                g_wait(L, k, q)
 
     f_sends = {1: has_far, 2: both(has_x, has_far), 4: has_x, 5: has_x}
     f_recvs = {1: has_cx, 2: both(has_x, has_cx), 4: has_x, 5: has_x}
 
-    def f_copy(L, k):
+    def f_copy(L, k, q):
+        part = pl.ds(q * CHUNK, CHUNK)
         src, dst, dev = {
-            0: (A.at[L, rcs], FC.at[L], (rc, c)),
-            1: (A.at[L, 1, fp], FX.at[L, 0], (r, cf)),
-            2: (A.at[L, rxs, fp], FX.at[L, 1], (r, cf)),
-            3: (A.at[L, 1, hp], FY.at[L, 0], (r, cp)),
-            4: (A.at[L, rxs, 1], FY.at[L, 1], (rx, c)),
-            5: (A.at[L, rxs, hp], FY.at[L, 2], (rx, cp)),
+            0: (A.at[L, rcs, fp, part], FC.at[L, fp, part], (rc, c)),
+            1: (A.at[L, 1, fp, part], FX.at[L, 0, part], (r, cf)),
+            2: (A.at[L, rxs, fp, part], FX.at[L, 1, part], (r, cf)),
+            3: (A.at[L, 1, hp, part], FY.at[L, 0, part], (r, cp)),
+            4: (A.at[L, rxs, 1, part], FY.at[L, 1, part], (rx, c)),
+            5: (A.at[L, rxs, hp, part], FY.at[L, 2, part], (rx, cp)),
+            6: (A.at[L, rcs, hp, part], FC.at[L, hp, part], (rc, c)),
+            7: (A.at[L, rcs, 1, part], FC.at[L, 1, part], (rc, c)),
         }[k]
         return pltpu.make_async_remote_copy(
             src_ref=src,
             dst_ref=dst,
-            send_sem=f_send.at[L, k],
-            recv_sem=f_recv.at[L, k],
+            send_sem=f_send.at[L, k, q],
+            recv_sem=f_recv.at[L, k, q],
             device_id={"rows": dev[0], "cols": dev[1]},
             device_id_type=MESH,
         )
 
-    def f_start(L, k):
-        when(f_sends.get(k, always), lambda: f_copy(L, k).start())
-
-    def f_wait(L, k):
-        when(f_recvs.get(k, always), lambda: f_copy(L, k).wait_recv())
-
-    def f_begin(planes):
-        for L in planes:
-            for k in (0, 2, 4):
-                f_start(L, k)
-
-    def f_core(planes):
-        for L in planes:
-            f_wait(L, 0)
-            A[L, 1, fp] += FC[L, fp]
-            f_start(L, 1)
-        for L in planes:
-            A[L, 1, hp] += FC[L, hp]
+    def f_start(L, k, q):
+        when(f_sends.get(k, always), lambda: f_copy(L, k, q).start())
+
+    def f_wait(L, k, q):
+        when(f_recvs.get(k, always), lambda: f_copy(L, k, q).wait_recv())
+
+    def f_begin(planes, kinds=(0, 4, 2, 6, 7)):
+        for k in kinds:
+            for L, q in chunks(planes):
+                f_start(L, k, q)
+
+    def f_core(planes, send=True):
+        for L, q in chunks(planes):
+            part = pl.ds(q * CHUNK, CHUNK)
+            f_wait(L, 0, q)
+            A[L, 1, fp, part] += FC[L, fp, part]
+            if send:
+                f_start(L, 1, q)
+        for L, q in chunks(planes):
+            part = pl.ds(q * CHUNK, CHUNK)
+            f_wait(L, 6, q)
+            A[L, 1, hp, part] += FC[L, hp, part]
 
     def f_across(planes):
-        for L in planes:
-            f_wait(L, 2)
+        for L, q in chunks(planes):
+            part = pl.ds(q * CHUNK, CHUNK)
+            f_wait(L, 2, q)
 
             @pl.when(f_recvs[2])
             def _():
-                A[L, rxs, hp] += FX[L, 1]
-
-            f_start(L, 5)
-            f_wait(L, 1)
+                A[L, rxs, hp, part] += FX[L, 1, part]
+
+            f_start(L, 5, q)
+        for L, q in chunks(planes):
+            part = pl.ds(q * CHUNK, CHUNK)
+            f_wait(L, 1, q)
 
             @pl.when(has_cx)
             def _():
-                A[L, 1, hp] += FX[L, 0]
-
-            f_start(L, 3)
-
-    def f_end(L):
-        f_wait(L, 3)
-        f_wait(L, 4)
-        f_wait(L, 5)
-        return A[L, 1, 1] + FC[L, 1] + FY[L, 0] + FY[L, 1] + FY[L, 2]
-
-    for plane in range(2):
-        G[plane, 1, 1] = obj_ref[plane]
+                A[L, 1, hp, part] += FX[L, 0, part]
+
+            f_start(L, 3, q)
+
+    def f_end(L, q):
+        part = pl.ds(q * CHUNK, CHUNK)
+        for k in (7, 4, 5, 3):
+            f_wait(L, k, q)
+        return A[L, 1, 1, part] + FC[L, 1, part] + FY[L, 0, part] + FY[L, 1, part] + FY[L, 2, part]
+
+    local[3].wait()
+    local[4].wait()
     greeted = 2 + 2 * has_x.astype(jnp.int32) + has_cx.astype(jnp.int32) + has_far.astype(jnp.int32)
     pl.semaphore_wait(barrier, greeted)
-    g_begin((0, 1))
+    g_begin((0, 1), (1, 2, 3, 0))
 
     zero_tile = jnp.zeros((T, T), f32)
 
@@ -250,8 +270,8 @@
     col_of = lax.broadcasted_iota(jnp.int32, (T, T), 1)
 
     def add_term(L, p, term):
-        mr = row_of >= off_ref[p, 0]
-        mc = col_of >= off_ref[p, 1]
+        mr = row_of >= off_ref[0, p]
+        mc = col_of >= off_ref[1, p]
         zero = jnp.zeros((T, T), f32)
         top = jnp.where(mr, term[0][0], zero)
         low = term[0][0] - top
@@ -273,14 +293,16 @@
     def roll_probe(p, carry):
         power = None
         for plane in range(2):
-            x = pltpu.roll(probe[plane], off_ref[p, 0], 0)
-            x = pltpu.roll(x, off_ref[p, 1], 1)
+            x = pltpu.roll(probe[plane], off_ref[0, p], 0)
+            x = pltpu.roll(x, off_ref[1, p], 1)
             rolled[p, plane] = x
             power = x * x if power is None else power + x * x
         add_term(2 * ITERS, p, blocks(power))
         return carry
 
     lax.fori_loop(0, n_pos, roll_probe, 0)
+    light = (2 * ITERS,)
+    f_begin(light, (0, 6, 7))
 
     local[1].wait()
     lane_in = lax.broadcasted_iota(jnp.int32, (W, W), 0)
@@ -312,8 +334,8 @@
         return mm(mats[m], hi) + mm(mats[m + 1], hi) + mm(mats[m], lo)
 
     def window(it, p):
-        mr = row_of >= off_ref[p, 0]
-        mc = col_of >= off_ref[p, 1]
+        mr = row_of >= off_ref[0, p]
+        mc = col_of >= off_ref[1, p]
         ob = []
         for L in (2 * it, 2 * it + 1):
             t = lambda a, b: G[L, a, b]
@@ -334,21 +356,25 @@
             vs.append(jnp.concatenate([er[0] - er[1], ei[0] - ei[1]], 1))
         even = right(jnp.concatenate(us, 0), 0)
         odd = right(jnp.concatenate(vs, 0), 2)
+        yield
         yr = jnp.concatenate([even[:, :T], odd[:, :T]], 1)
         yi = jnp.concatenate([even[:, T:], odd[:, T:]], 1)
         u = jnp.concatenate([yr[:T] + yr[T:], yi[:T] + yi[T:]], 0)
         v = jnp.concatenate([yr[:T] - yr[T:], yi[:T] - yi[T:]], 0)
         back = []
-        for par, x in ((0, u), (1, v)):
-            far = left(4 + 2 * par, x)
+        fars = [left(4 + 2 * par, x) for par, x in ((0, u), (1, v))]
+        yield
+        for par, far in enumerate(fars):
             fr, fi = far[:T], far[T:]
             keep = 1.0 - ampp[p, par] * lax.rsqrt(jnp.maximum(fr * fr + fi * fi, 0.25))
             back.append(left(2 * par, jnp.concatenate([fr * keep, fi * keep], 0)))
+        yield
         tot, dif = back[0] + back[1], back[0] - back[1]
         zr = jnp.concatenate([tot[:T], dif[:T]], 0)
         zi = jnp.concatenate([tot[T:], dif[T:]], 0)
         even = right(jnp.concatenate([zr[:, :T], zi[:, :T]], 1), 4)
         odd = right(jnp.concatenate([zr[:, T:], zi[:, T:]], 1), 6)
+        yield
         tot, dif = even + odd, even - odd
         tr, ti = [], []
         for i in range(2):
@@ -359,61 +385,70 @@
             ti.append([pr[i][j] * bi[j] - pi[i][j] * br[j] for j in range(2)])
         add_term(2 * it, p, tr)
         add_term(2 * it + 1, p, ti)
+        yield
 
     def windows(it, first, last):
-        def step(p, carry):
-            window(it, p)
+        def step(t, carry):
+            running = [window(it, first + GROUP * t + i) for i in range(GROUP)]
+            for _ in range(5):
+                for one in running:
+                    next(one)
             return carry
 
-        lax.fori_loop(first, last, step, 0)
+        lax.fori_loop(0, (last - first) // GROUP, step, 0)
 
     g_finish((0, 1))
-    light = (2 * ITERS,)
-    f_begin(light)
+    f_core(light, False)
+    f_begin(light, (4, 2, 1))
     for it in range(ITERS):
+        planes = (2 * it, 2 * it + 1)
         if it == 0:
             half = n_pos // 2
             windows(it, 0, half)
-            f_core(light)
+            f_across(light)
             windows(it, half, n_pos)
         else:
             windows(it, 0, n_pos)
-        planes = (2 * it, 2 * it + 1)
         f_begin(planes)
         if it == 0:
-            f_across(light)
+            for _, q in chunks(light):
+                ill[pl.ds(q * CHUNK, CHUNK)] = f_end(2 * ITERS, q) + 1.0
         f_core(planes)
         f_across(planes)
-        if it == 0:
-            ill[...] = f_end(2 * ITERS) + 1.0
-        for plane in range(2):
-            L = 2 * it + plane
-            new = G[L, 1, 1] - f_end(L) / ill[...]
+        for L, q in chunks(planes):
+            part = pl.ds(q * CHUNK, CHUNK)
+            new = G[L, 1, 1, part] - f_end(L, q) / ill[part]
             if it < ITERS - 1:
-                G[L + 2, 1, 1] = new
-                g_begin((L + 2,))
+                G[L + 2, 1, 1, part] = new
+                g_start(L + 2, 1, q)
             else:
-                out_ref[plane] = new
+                out_ref[L - 2 * it, part] = new
         if it < ITERS - 1:
-            g_finish((2 * it + 2, 2 * it + 3))
-
-    for L in range(2 * ITERS):
+            planes = (2 * it + 2, 2 * it + 3)
+            g_begin(planes, (2, 3, 0))
+            g_finish(planes)
+
+    for L, q in chunks(range(2 * ITERS)):
         for k in range(8):
-            when(g_sends.get(k, always), lambda L=L, k=k: g_copy(L, k).wait_send())
-    for L in range(2 * ITERS + 1):
-        for k in range(6):
-            when(f_sends.get(k, always), lambda L=L, k=k: f_copy(L, k).wait_send())
+            when(g_sends.get(k, always), lambda: g_copy(L, k, q).wait_send())
+    for L, q in chunks(range(2 * ITERS + 1)):
+        for k in range(8):
+            when(f_sends.get(k, always), lambda: f_copy(L, k, q).wait_send())
 
 
 def local(n_rows, n_cols, object_field, probe, amplitudes, offsets):
     n_pos = amplitudes.shape[2]
     n = 2 * ITERS
-    anyspace = pl.BlockSpec(memory_space=pl.ANY)
+
+    def fix(x):
+        return pltpu.with_memory_space_constraint(x, pltpu.HBM)
+
+    hbm = pl.BlockSpec(memory_space=pltpu.HBM)
     vmem = pl.BlockSpec(memory_space=pltpu.VMEM)
     return pl.pallas_call(
         functools.partial(kernel, n_rows, n_cols, n_pos),
         out_shape=jax.ShapeDtypeStruct(object_field.shape, f32),
-        in_specs=[vmem, pl.BlockSpec(memory_space=pltpu.SMEM), anyspace, anyspace, anyspace],
+        in_specs=[hbm, pl.BlockSpec(memory_space=pltpu.SMEM), hbm, hbm, hbm],
         out_specs=vmem,
         scratch_shapes=[
             pltpu.VMEM((n, 3, 3, T, T), f32),
@@ -428,21 +463,21 @@
             pltpu.VMEM((n_pos, 2, W, W), f32),
             pltpu.VMEM((n_pos, 2, T, W), f32),
             pltpu.VMEM((2, W, T), f32),
-            pltpu.SemaphoreType.DMA((n, 8)),
-            pltpu.SemaphoreType.DMA((n, 8)),
-            pltpu.SemaphoreType.DMA((n + 1, 6)),
-            pltpu.SemaphoreType.DMA((n + 1, 6)),
-            pltpu.SemaphoreType.DMA((3,)),
+            pltpu.SemaphoreType.DMA((n, 8, T // CHUNK)),
+            pltpu.SemaphoreType.DMA((n, 8, T // CHUNK)),
+            pltpu.SemaphoreType.DMA((n + 1, 8, T // CHUNK)),
+            pltpu.SemaphoreType.DMA((n + 1, 8, T // CHUNK)),
+            pltpu.SemaphoreType.DMA((5,)),
         ],
         compiler_params=pltpu.CompilerParams(
-            collective_id=0, has_side_effects=True, vmem_limit_bytes=56 * 1024 * 1024
+            collective_id=0, has_side_effects=True, vmem_limit_bytes=VMEM_MIB * 1024 * 1024
         ),
     )(
-        object_field,
-        offsets[0, 0],
-        probe,
-        amplitudes[0, 0],
-        jnp.asarray(dft_parts()),
+        fix(object_field),
+        fix(offsets[0, 0].T),
+        fix(probe),
+        fix(amplitudes[0, 0]),
+        fix(jnp.asarray(dft_parts())),
     )
 
 

time: 70.5 us -> 62.1 us (0.88)
  Pallas kernels: 67 us -> 60.9 us
  local copies, waits for them, and re-layouts: 2.91 us -> 0.66 us
    pallas_call x1, Pallas kernels: 67 us -> 60.9 us  [local(): pl.pallas_call(functools.partial(kernel, n_rows, n_cols, n_pos), out_shap...]
    unnamed x3 -> x1, local copies, waits for them, and re-layouts: 2.25 us -> 0.66 us
where the time goes in v1:
time: 62.1 us; the launch traced here: 61.6 us
  Pallas kernels  60.9 us (98%)
  local copies, waits for them, and re-layouts  0.66 us (1%)
    pallas_call x1, Pallas kernels, local(): pl.pallas_call(functools.partial(kernel, n_rows, n_cols, n_pos), out_shap...  60.9 us

profile of v1, /device:TPU:96, one launch (start us, length us, event | category | flops | bytes accessed | tf_op | source)
XLA Modules:
  0.0 61.6 jit_solution(17729768389132291319)
XLA Ops:
  0.0 60.9 %shard_map.55 = f32[2,128,128]{2,1,0:T(8,128)S(1)} custom-call(f32[2,128,128]{2,1,0:T(8,128)} %obj_hbm.1, s32[2,4]{1,0:T(2,128)} %bitcast.5, f32[2,256,256]{2,1,0:T(8,128)} %probe_hbm.1, f32[4,256,256]{2,1,0:T(8,128)} %bitcast.4, bf16[8,256,256]{2,1,0:T(8,128)(2,1)} %constant.2.clone.mats_hbm), custom_call_target="tpu_custom_call" | custom-call | tf_op jit(solution)/shard_map/pallas_call | solution.py:448
  60.9 0.7 %copy.7 = f32[2,128,128]{2,1,0:T(8,128)} copy(f32[2,128,128]{2,1,0:T(8,128)S(1)} %shard_map.55) | data formatting | bytes 262144

commit v2 on v1

--- a/solution.py
+++ b/solution.py
@@ -51,7 +51,7 @@
     n_rows, n_cols, n_pos,
     obj_hbm, off_ref, probe_hbm, amp_hbm, mats_hbm,
     out_ref,
-    G, A, FC, FX, FY, ill, probe, amp, mats, rolled, ampp, halves,
+    G, A, FC, FR, FX, FY, ill, probe, amp, mats, rolled, ampp, halves, held,
     g_send, g_recv, f_send, f_recv, l_sem,
 ):
     r = lax.axis_index("rows")
@@ -91,7 +91,6 @@
     @pl.when(has_x)
     def _():
         greet(rx, c)
-        greet(rx, cp)
 
     @pl.when(has_cx)
     def _():
@@ -112,7 +111,7 @@
         else:
             pl.when(cond)(f)
 
-    g_sends = {2: has_x, 3: has_x, 4: has_cx, 5: both(has_x, has_cx), 7: has_far}
+    g_sends = {2: has_x, 3: has_x, 4: has_cx, 5: both(has_x, has_far), 7: has_far}
     g_recvs = {2: has_x, 3: has_x, 4: has_far, 5: both(has_x, has_far), 7: has_far}
 
     def g_copy(L, k, q):
@@ -120,9 +119,9 @@
             0: ((1, 1), (2 - rcs, 1), (rc, c)),
             1: ((1, 1), (1, 2 - hp), (r, cp)),
             2: ((1, 1), (2 - rxs, 1), (rx, c)),
-            3: ((1, 1), (2 - rxs, 2 - hp), (rx, cp)),
+            3: ((1, hp), (2 - rxs, hp), (rx, c)),
             4: ((1, hp), (1, fp), (r, cx)),
-            5: ((rxs, hp), (rxs, fp), (r, cx)),
+            5: ((1, fp), (2 - rxs, fp), (rx, c)),
             6: ((1, hp), (2 - rcs, hp), (rc, c)),
             7: ((1, fp), (2 - rcs, fp), (rc, c)),
         }[k]
@@ -145,40 +144,65 @@
     def chunks(planes):
         return [(L, q) for L in planes for q in range(T // CHUNK)]
 
+    def start_all(copy, sends, planes, k):
+        def go():
+            for L, q in chunks(planes):
+                copy(L, k, q).start()
+
+        when(sends.get(k, always), go)
+
     def g_begin(planes, kinds):
         for k in kinds:
-            for L, q in chunks(planes):
-                g_start(L, k, q)
-
-    def g_finish(planes):
+            start_all(g_copy, g_sends, planes, k)
+
+    def g_finish(it, meanwhile=None):
+        planes = (2 * it, 2 * it + 1)
         for L, q in chunks(planes):
             g_wait(L, 1, q)
             g_start(L, 4, q)
             g_start(L, 6, q)
+            g_start(L, 3, q)
+        if meanwhile is not None:
+            meanwhile()
+
+        @pl.when(has_far)
+        def _():
+            for L, q in chunks(planes):
+                g_copy(L, 4, q).wait_recv()
+                g_copy(L, 7, q).start()
+                g_start(L, 5, q)
+
+        every(before, 2, it)
         for L, q in chunks(planes):
-            g_wait(L, 3, q)
-            g_start(L, 5, q)
-        for L, q in chunks(planes):
-            g_wait(L, 4, q)
-            g_start(L, 7, q)
-        for k in (0, 2, 5, 6, 7):
+            g_wait(L, 0, q)
+            g_wait(L, 6, q)
+
+        @pl.when(has_x)
+        def _():
             for L, q in chunks(planes):
-                g_wait(L, k, q)
-
-    f_sends = {1: has_far, 2: both(has_x, has_far), 4: has_x, 5: has_x}
-    f_recvs = {1: has_cx, 2: both(has_x, has_cx), 4: has_x, 5: has_x}
+                g_copy(L, 2, q).wait_recv()
+                g_copy(L, 3, q).wait_recv()
+
+        @pl.when(has_far)
+        def _():
+            for L, q in chunks(planes):
+                g_copy(L, 7, q).wait_recv()
+                g_wait(L, 5, q)
+
+    f_sends = {1: has_far, 2: has_x, 4: has_x, 5: has_x}
+    f_recvs = {1: has_cx, 2: has_x, 4: has_x, 5: has_x}
 
     def f_copy(L, k, q):
         part = pl.ds(q * CHUNK, CHUNK)
         src, dst, dev = {
             0: (A.at[L, rcs, fp, part], FC.at[L, fp, part], (rc, c)),
-            1: (A.at[L, 1, fp, part], FX.at[L, 0, part], (r, cf)),
-            2: (A.at[L, rxs, fp, part], FX.at[L, 1, part], (r, cf)),
-            3: (A.at[L, 1, hp, part], FY.at[L, 0, part], (r, cp)),
-            4: (A.at[L, rxs, 1, part], FY.at[L, 1, part], (rx, c)),
-            5: (A.at[L, rxs, hp, part], FY.at[L, 2, part], (rx, cp)),
             6: (A.at[L, rcs, hp, part], FC.at[L, hp, part], (rc, c)),
             7: (A.at[L, rcs, 1, part], FC.at[L, 1, part], (rc, c)),
+            2: (A.at[L, rxs, fp, part], FR.at[L, fp, part], (rx, c)),
+            5: (A.at[L, rxs, hp, part], FR.at[L, hp, part], (rx, c)),
+            4: (A.at[L, rxs, 1, part], FR.at[L, 1, part], (rx, c)),
+            1: (A.at[L, 1, fp, part], FX.at[L, part], (r, cf)),
+            3: (A.at[L, 1, hp, part], FY.at[L, part], (r, cp)),
         }[k]
         return pltpu.make_async_remote_copy(
             src_ref=src,
@@ -195,54 +219,41 @@
     def f_wait(L, k, q):
         when(f_recvs.get(k, always), lambda: f_copy(L, k, q).wait_recv())
 
-    def f_begin(planes, kinds=(0, 4, 2, 6, 7)):
+    def f_begin(planes, kinds=(0, 2, 6, 5, 7, 4)):
         for k in kinds:
-            for L, q in chunks(planes):
-                f_start(L, k, q)
-
-    def f_core(planes, send=True):
+            start_all(f_copy, f_sends, planes, k)
+
+    def f_core(planes):
         for L, q in chunks(planes):
             part = pl.ds(q * CHUNK, CHUNK)
             f_wait(L, 0, q)
-            A[L, 1, fp, part] += FC[L, fp, part]
-            if send:
-                f_start(L, 1, q)
+            f_wait(L, 2, q)
+            A[L, 1, fp, part] += FC[L, fp, part] + FR[L, fp, part]
+            f_start(L, 1, q)
         for L, q in chunks(planes):
             part = pl.ds(q * CHUNK, CHUNK)
             f_wait(L, 6, q)
-            A[L, 1, hp, part] += FC[L, hp, part]
+            f_wait(L, 5, q)
+            A[L, 1, hp, part] += FC[L, hp, part] + FR[L, hp, part]
 
     def f_across(planes):
         for L, q in chunks(planes):
             part = pl.ds(q * CHUNK, CHUNK)
-            f_wait(L, 2, q)
-
-            @pl.when(f_recvs[2])
-            def _():
-                A[L, rxs, hp, part] += FX[L, 1, part]
-
-            f_start(L, 5, q)
-        for L, q in chunks(planes):
-            part = pl.ds(q * CHUNK, CHUNK)
             f_wait(L, 1, q)
-
-            @pl.when(has_cx)
-            def _():
-                A[L, 1, hp, part] += FX[L, 0, part]
-
+            A[L, 1, hp, part] += FX[L, part]
             f_start(L, 3, q)
 
     def f_end(L, q):
         part = pl.ds(q * CHUNK, CHUNK)
-        for k in (7, 4, 5, 3):
+        for k in (7, 4, 3):
             f_wait(L, k, q)
-        return A[L, 1, 1, part] + FC[L, 1, part] + FY[L, 0, part] + FY[L, 1, part] + FY[L, 2, part]
+        return A[L, 1, 1, part] + FC[L, 1, part] + FR[L, 1, part] + FY[L, part]
 
     local[3].wait()
     local[4].wait()
-    greeted = 2 + 2 * has_x.astype(jnp.int32) + has_cx.astype(jnp.int32) + has_far.astype(jnp.int32)
+    greeted = 2 + has_x.astype(jnp.int32) + has_cx.astype(jnp.int32) + has_far.astype(jnp.int32)
     pl.semaphore_wait(barrier, greeted)
-    g_begin((0, 1), (1, 2, 3, 0))
+    g_begin((0, 1), (1, 2, 0))
 
     zero_tile = jnp.zeros((T, T), f32)
 
@@ -252,8 +263,13 @@
             for col in range(3):
                 G[L, rxs, col] = zero_tile
         for L in range(2 * ITERS + 1):
-            FY[L, 1] = zero_tile
-            FY[L, 2] = zero_tile
+            for col in range(3):
+                FR[L, col] = zero_tile
+
+    @pl.when(jnp.logical_not(has_cx))
+    def _():
+        for L in range(2 * ITERS + 1):
+            FX[L] = zero_tile
 
     @pl.when(jnp.logical_not(has_far))
     def _():
@@ -269,24 +285,23 @@
     row_of = lax.broadcasted_iota(jnp.int32, (T, T), 0)
     col_of = lax.broadcasted_iota(jnp.int32, (T, T), 1)
 
-    def add_term(L, p, term):
+    def add_rows(L, p, i, term):
         mr = row_of >= off_ref[0, p]
         mc = col_of >= off_ref[1, p]
         zero = jnp.zeros((T, T), f32)
-        top = jnp.where(mr, term[0][0], zero)
-        low = term[0][0] - top
-        A[L, 0, 0] += jnp.where(mc, top, zero)
-        A[L, 0, 2] += jnp.where(mc, zero, top)
-        A[L, 2, 0] += jnp.where(mc, low, zero)
-        A[L, 2, 2] += jnp.where(mc, zero, low)
-        A[L, 0, 1] += jnp.where(mr, term[0][1], zero)
-        A[L, 2, 1] += jnp.where(mr, zero, term[0][1])
-        A[L, 1, 0] += jnp.where(mc, term[1][0], zero)
-        A[L, 1, 2] += jnp.where(mc, zero, term[1][0])
-        A[L, 1, 1] += term[1][1]
-
-    def blocks(x):
-        return [[x[i * T:(i + 1) * T, j * T:(j + 1) * T] for j in range(2)] for i in range(2)]
+        if i == 0:
+            top = jnp.where(mr, term[0], zero)
+            low = jnp.where(mr, zero, term[0])
+            A[L, 0, 0] += jnp.where(mc, top, zero)
+            A[L, 0, 2] += jnp.where(mc, zero, top)
+            A[L, 2, 0] += jnp.where(mc, low, zero)
+            A[L, 2, 2] += jnp.where(mc, zero, low)
+            A[L, 0, 1] += jnp.where(mr, term[1], zero)
+            A[L, 2, 1] += jnp.where(mr, zero, term[1])
+        else:
+            A[L, 1, 0] += jnp.where(mc, term[0], zero)
+            A[L, 1, 2] += jnp.where(mc, zero, term[0])
+            A[L, 1, 1] += term[1]
 
     local[0].wait()
 
@@ -297,12 +312,14 @@
             x = pltpu.roll(x, off_ref[1, p], 1)
             rolled[p, plane] = x
             power = x * x if power is None else power + x * x
-        add_term(2 * ITERS, p, blocks(power))
+        for i in range(2):
+            rows = power[i * T:(i + 1) * T]
+            add_rows(2 * ITERS, p, i, [rows[:, :T], rows[:, T:]])
         return carry
 
     lax.fori_loop(0, n_pos, roll_probe, 0)
     light = (2 * ITERS,)
-    f_begin(light, (0, 6, 7))
+    f_begin(light)
 
     local[1].wait()
     lane_in = lax.broadcasted_iota(jnp.int32, (W, W), 0)
@@ -333,34 +350,60 @@
         hi, lo = split(x)
         return mm(mats[m], hi) + mm(mats[m + 1], hi) + mm(mats[m], lo)
 
-    def window(it, p):
+    def exit_rows(it, p, i):
         mr = row_of >= off_ref[0, p]
         mc = col_of >= off_ref[1, p]
         ob = []
         for L in (2 * it, 2 * it + 1):
             t = lambda a, b: G[L, a, b]
-            ob.append([
-                [
+            if i == 0:
+                ob.append([
                     jnp.where(mr, jnp.where(mc, t(0, 0), t(0, 2)), jnp.where(mc, t(2, 0), t(2, 2))),
                     jnp.where(mr, t(0, 1), t(2, 1)),
-                ],
-                [jnp.where(mc, t(1, 0), t(1, 2)), t(1, 1)],
-            ])
-        pr = blocks(rolled[p, 0])
-        pi = blocks(rolled[p, 1])
-        us, vs = [], []
-        for i in range(2):
-            er = [pr[i][j] * ob[0][i][j] - pi[i][j] * ob[1][i][j] for j in range(2)]
-            ei = [pr[i][j] * ob[1][i][j] + pi[i][j] * ob[0][i][j] for j in range(2)]
-            us.append(jnp.concatenate([er[0] + er[1], ei[0] + ei[1]], 1))
-            vs.append(jnp.concatenate([er[0] - er[1], ei[0] - ei[1]], 1))
-        even = right(jnp.concatenate(us, 0), 0)
-        odd = right(jnp.concatenate(vs, 0), 2)
-        yield
-        yr = jnp.concatenate([even[:, :T], odd[:, :T]], 1)
-        yi = jnp.concatenate([even[:, T:], odd[:, T:]], 1)
-        u = jnp.concatenate([yr[:T] + yr[T:], yi[:T] + yi[T:]], 0)
-        v = jnp.concatenate([yr[:T] - yr[T:], yi[:T] - yi[T:]], 0)
+                ])
+            else:
+                ob.append([jnp.where(mc, t(1, 0), t(1, 2)), t(1, 1)])
+        rows = slice(i * T, (i + 1) * T)
+        pr = [rolled[p, 0, rows, :T], rolled[p, 0, rows, T:]]
+        pi = [rolled[p, 1, rows, :T], rolled[p, 1, rows, T:]]
+        er = [pr[j] * ob[0][j] - pi[j] * ob[1][j] for j in range(2)]
+        ei = [pr[j] * ob[1][j] + pi[j] * ob[0][j] for j in range(2)]
+        u = jnp.concatenate([er[0] + er[1], ei[0] + ei[1]], 1)
+        v = jnp.concatenate([er[0] - er[1], ei[0] - ei[1]], 1)
+        return right(u, 0), right(v, 2)
+
+    def back_rows(zr, zi):
+        even = right(jnp.concatenate([zr[:, :T], zi[:, :T]], 1), 4)
+        odd = right(jnp.concatenate([zr[:, T:], zi[:, T:]], 1), 6)
+        return even, odd
+
+    def terms(p, i, even, odd):
+        tot, dif = even + odd, even - odd
+        br = [tot[:, :T], dif[:, :T]]
+        bi = [tot[:, T:], dif[:, T:]]
+        rows = slice(i * T, (i + 1) * T)
+        pr = [rolled[p, 0, rows, :T], rolled[p, 0, rows, T:]]
+        pi = [rolled[p, 1, rows, :T], rolled[p, 1, rows, T:]]
+        return (
+            [pr[j] * br[j] + pi[j] * bi[j] for j in range(2)],
+            [pr[j] * bi[j] - pi[j] * br[j] for j in range(2)],
+        )
+
+    def before(it, p):
+        even, odd = exit_rows(it, p, 1)
+        yield
+        held[p, 0] = even
+        held[p, 1] = odd
+        yield
+
+    def window(it, p):
+        even, odd = exit_rows(it, p, 0)
+        yield
+        low_even, low_odd = held[p, 0], held[p, 1]
+        yr = [jnp.concatenate([e[:, :T], o[:, :T]], 1) for e, o in ((even, odd), (low_even, low_odd))]
+        yi = [jnp.concatenate([e[:, T:], o[:, T:]], 1) for e, o in ((even, odd), (low_even, low_odd))]
+        u = jnp.concatenate([yr[0] + yr[1], yi[0] + yi[1]], 0)
+        v = jnp.concatenate([yr[0] - yr[1], yi[0] - yi[1]], 0)
         back = []
         fars = [left(4 + 2 * par, x) for par, x in ((0, u), (1, v))]
         yield
@@ -370,46 +413,38 @@
             back.append(left(2 * par, jnp.concatenate([fr * keep, fi * keep], 0)))
         yield
         tot, dif = back[0] + back[1], back[0] - back[1]
-        zr = jnp.concatenate([tot[:T], dif[:T]], 0)
-        zi = jnp.concatenate([tot[T:], dif[T:]], 0)
-        even = right(jnp.concatenate([zr[:, :T], zi[:, :T]], 1), 4)
-        odd = right(jnp.concatenate([zr[:, T:], zi[:, T:]], 1), 6)
-        yield
-        tot, dif = even + odd, even - odd
-        tr, ti = [], []
-        for i in range(2):
-            rows = slice(i * T, (i + 1) * T)
-            br = [tot[rows, :T], dif[rows, :T]]
-            bi = [tot[rows, T:], dif[rows, T:]]
-            tr.append([pr[i][j] * br[j] + pi[i][j] * bi[j] for j in range(2)])
-            ti.append([pr[i][j] * bi[j] - pi[i][j] * br[j] for j in range(2)])
-        add_term(2 * it, p, tr)
-        add_term(2 * it + 1, p, ti)
-        yield
-
-    def windows(it, first, last):
+        held[p, 0] = dif[:T]
+        held[p, 1] = dif[T:]
+        even, odd = back_rows(tot[:T], tot[T:])
+        yield
+        for L, term in zip((2 * it, 2 * it + 1), terms(p, 0, even, odd)):
+            add_rows(L, p, 0, term)
+        yield
+
+    def after(it, p):
+        even, odd = back_rows(held[p, 0], held[p, 1])
+        yield
+        for L, term in zip((2 * it, 2 * it + 1), terms(p, 1, even, odd)):
+            add_rows(L, p, 1, term)
+        yield
+
+    def every(part, stages, it):
         def step(t, carry):
-            running = [window(it, first + GROUP * t + i) for i in range(GROUP)]
-            for _ in range(5):
+            running = [part(it, GROUP * t + i) for i in range(GROUP)]
+            for _ in range(stages):
                 for one in running:
                     next(one)
             return carry
 
-        lax.fori_loop(0, (last - first) // GROUP, step, 0)
-
-    g_finish((0, 1))
-    f_core(light, False)
-    f_begin(light, (4, 2, 1))
+        lax.fori_loop(0, n_pos // GROUP, step, 0)
+
+    g_finish(0, lambda: f_core(light))
+    f_across(light)
     for it in range(ITERS):
         planes = (2 * it, 2 * it + 1)
-        if it == 0:
-            half = n_pos // 2
-            windows(it, 0, half)
-            f_across(light)
-            windows(it, half, n_pos)
-        else:
-            windows(it, 0, n_pos)
+        every(window, 5, it)
         f_begin(planes)
+        every(after, 2, it)
         if it == 0:
             for _, q in chunks(light):
                 ill[pl.ds(q * CHUNK, CHUNK)] = f_end(2 * ITERS, q) + 1.0
@@ -425,15 +460,17 @@
                 out_ref[L - 2 * it, part] = new
         if it < ITERS - 1:
             planes = (2 * it + 2, 2 * it + 3)
-            g_begin(planes, (2, 3, 0))
-            g_finish(planes)
-
-    for L, q in chunks(range(2 * ITERS)):
+            g_begin(planes, (2, 0))
+            g_finish(it + 1)
+
+    for copy, sends, planes in ((g_copy, g_sends, 2 * ITERS), (f_copy, f_sends, 2 * ITERS + 1)):
         for k in range(8):
-            when(g_sends.get(k, always), lambda: g_copy(L, k, q).wait_send())
-    for L, q in chunks(range(2 * ITERS + 1)):
-        for k in range(8):
-            when(f_sends.get(k, always), lambda: f_copy(L, k, q).wait_send())
+
+            def drain():
+                for L, q in chunks(range(planes)):
+                    copy(L, k, q).wait_send()
+
+            when(sends.get(k, always), drain)
 
 
 def local(n_rows, n_cols, object_field, probe, amplitudes, offsets):
@@ -454,8 +491,9 @@
             pltpu.VMEM((n, 3, 3, T, T), f32),
             pltpu.VMEM((n + 1, 3, 3, T, T), f32),
             pltpu.VMEM((n + 1, 3, T, T), f32),
-            pltpu.VMEM((n + 1, 2, T, T), f32),
             pltpu.VMEM((n + 1, 3, T, T), f32),
+            pltpu.VMEM((n + 1, T, T), f32),
+            pltpu.VMEM((n + 1, T, T), f32),
             pltpu.VMEM((T, T), f32),
             pltpu.VMEM((2, W, W), f32),
             pltpu.VMEM((n_pos, W, W), f32),
@@ -463,6 +501,7 @@
             pltpu.VMEM((n_pos, 2, W, W), f32),
             pltpu.VMEM((n_pos, 2, T, W), f32),
             pltpu.VMEM((2, W, T), f32),
+            pltpu.VMEM((n_pos, 2, T, W), f32),
             pltpu.SemaphoreType.DMA((n, 8, T // CHUNK)),
             pltpu.SemaphoreType.DMA((n, 8, T // CHUNK)),
             pltpu.SemaphoreType.DMA((n + 1, 8, T // CHUNK)),

time: 62.1 us -> 59.5 us (0.958)
  Pallas kernels: 60.9 us -> 58.7 us
    pallas_call x1, Pallas kernels: 60.9 us -> 58.7 us  [local(): pl.pallas_call(functools.partial(kernel, n_rows, n_cols, n_pos), out_shap...]
where the time goes in v2:
time: 59.5 us; the launch traced here: 59.4 us
  Pallas kernels  58.7 us (99%)
  local copies, waits for them, and re-layouts  0.66 us (1%)
    pallas_call x1, Pallas kernels, local(): pl.pallas_call(functools.partial(kernel, n_rows, n_cols, n_pos), out_shap...  58.7 us

profile of v2, /device:TPU:96, one launch (start us, length us, event | category | flops | bytes accessed | tf_op | source)
XLA Modules:
  0.0 59.4 jit_solution(6759978472880983764)
XLA Ops:
  0.0 58.7 %shard_map.55 = f32[2,128,128]{2,1,0:T(8,128)S(1)} custom-call(f32[2,128,128]{2,1,0:T(8,128)} %obj_hbm.1, s32[2,4]{1,0:T(2,128)} %bitcast.5, f32[2,256,256]{2,1,0:T(8,128)} %probe_hbm.1, f32[4,256,256]{2,1,0:T(8,128)} %bitcast.4, bf16[8,256,256]{2,1,0:T(8,128)(2,1)} %constant.2.clone.mats_hbm), custom_call_target="tpu_custom_call" | custom-call | tf_op jit(solution)/shard_map/pallas_call | solution.py:485
  58.7 0.7 %copy.7 = f32[2,128,128]{2,1,0:T(8,128)} copy(f32[2,128,128]{2,1,0:T(8,128)S(1)} %shard_map.55) | data formatting | bytes 262144

commit v3 on v2

--- a/solution.py
+++ b/solution.py
@@ -13,7 +13,7 @@
 T = 128
 W = 256
 CHUNK = 64
-GROUP = 2
+GROUP = 4
 VMEM_MIB = 28
 MESH = pl.DeviceIdType.MESH
 f32 = jnp.float32
@@ -111,10 +111,29 @@
         else:
             pl.when(cond)(f)
 
+    def tile(ph, L, q):
+        if L is None:
+            n = 2 if ph < ITERS else 1
+            return pl.ds(2 * ph, n), ()
+        return L, (pl.ds(q * CHUNK, CHUNK),)
+
+    def chunks(ph):
+        n = 2 if ph < ITERS else 1
+        return [(2 * ph + i, q) for i in range(n) for q in range(T // CHUNK)]
+
+    def remote(src, dst, send, recv, ph, L, q, k, dev):
+        return pltpu.make_async_remote_copy(
+            src_ref=src,
+            dst_ref=dst,
+            send_sem=send.at[ph, k],
+            recv_sem=recv.at[2 * ph, k, 0] if L is None else recv.at[L, k, q],
+            device_id={"rows": dev[0], "cols": dev[1]},
+            device_id_type=MESH,
+        )
+
     g_sends = {2: has_x, 3: has_x, 4: has_cx, 5: both(has_x, has_far), 7: has_far}
-    g_recvs = {2: has_x, 3: has_x, 4: has_far, 5: both(has_x, has_far), 7: has_far}
-
-    def g_copy(L, k, q):
+
+    def g_copy(ph, k, L=None, q=None):
         src, dst, dev = {
             0: ((1, 1), (2 - rcs, 1), (rc, c)),
             1: ((1, 1), (1, 2 - hp), (r, cp)),
@@ -125,135 +144,116 @@
             6: ((1, hp), (2 - rcs, hp), (rc, c)),
             7: ((1, fp), (2 - rcs, fp), (rc, c)),
         }[k]
-        part = (pl.ds(q * CHUNK, CHUNK),)
-        return pltpu.make_async_remote_copy(
-            src_ref=G.at[(L,) + src + part],
-            dst_ref=G.at[(L,) + dst + part],
-            send_sem=g_send.at[L, k, q],
-            recv_sem=g_recv.at[L, k, q],
-            device_id={"rows": dev[0], "cols": dev[1]},
-            device_id_type=MESH,
+        lead, part = tile(ph, L, q)
+        return remote(
+            G.at[(lead,) + src + part], G.at[(lead,) + dst + part], g_send, g_recv, ph, L, q, k, dev
         )
 
-    def g_start(L, k, q):
-        when(g_sends.get(k, always), lambda: g_copy(L, k, q).start())
-
-    def g_wait(L, k, q):
-        when(g_recvs.get(k, always), lambda: g_copy(L, k, q).wait_recv())
-
-    def chunks(planes):
-        return [(L, q) for L in planes for q in range(T // CHUNK)]
-
-    def start_all(copy, sends, planes, k):
-        def go():
-            for L, q in chunks(planes):
-                copy(L, k, q).start()
-
-        when(sends.get(k, always), go)
-
-    def g_begin(planes, kinds):
-        for k in kinds:
-            start_all(g_copy, g_sends, planes, k)
-
-    def g_finish(it, meanwhile=None):
-        planes = (2 * it, 2 * it + 1)
-        for L, q in chunks(planes):
-            g_wait(L, 1, q)
-            g_start(L, 4, q)
-            g_start(L, 6, q)
-            g_start(L, 3, q)
+    def g_begin(ph):
+        g_copy(ph, 0).start()
+        pl.when(has_x)(lambda: g_copy(ph, 2).start())
+
+    def g_finish(ph, meanwhile=None):
+        for L, q in chunks(ph):
+            g_copy(ph, 1, L, q).wait_recv()
+            pl.when(has_cx)(lambda: g_copy(ph, 4, L, q).start())
+        g_copy(ph, 6).start()
+        pl.when(has_x)(lambda: g_copy(ph, 3).start())
         if meanwhile is not None:
             meanwhile()
 
         @pl.when(has_far)
         def _():
-            for L, q in chunks(planes):
-                g_copy(L, 4, q).wait_recv()
-                g_copy(L, 7, q).start()
-                g_start(L, 5, q)
-
-        every(before, 2, it)
-        for L, q in chunks(planes):
-            g_wait(L, 0, q)
-            g_wait(L, 6, q)
+            for L, q in chunks(ph):
+                g_copy(ph, 4, L, q).wait_recv()
+                pl.when(has_x)(lambda: g_copy(ph, 5, L, q).start())
+                g_copy(ph, 7, L, q).start()
+
+        every(before, 2, ph)
+        g_copy(ph, 0).wait_recv()
+        g_copy(ph, 6).wait_recv()
 
         @pl.when(has_x)
         def _():
-            for L, q in chunks(planes):
-                g_copy(L, 2, q).wait_recv()
-                g_copy(L, 3, q).wait_recv()
+            g_copy(ph, 2).wait_recv()
+            g_copy(ph, 3).wait_recv()
 
         @pl.when(has_far)
         def _():
-            for L, q in chunks(planes):
-                g_copy(L, 7, q).wait_recv()
-                g_wait(L, 5, q)
+            for L, q in chunks(ph):
+                g_copy(ph, 7, L, q).wait_recv()
+                pl.when(has_x)(lambda: g_copy(ph, 5, L, q).wait_recv())
 
     f_sends = {1: has_far, 2: has_x, 4: has_x, 5: has_x}
-    f_recvs = {1: has_cx, 2: has_x, 4: has_x, 5: has_x}
-
-    def f_copy(L, k, q):
+
+    def f_copy(ph, k, L=None, q=None):
+        lead, part = tile(ph, L, q)
+        src, dst, dev = {
+            0: (A.at[(lead, rcs, fp) + part], FC.at[(lead, fp) + part], (rc, c)),
+            6: (A.at[(lead, rcs, hp) + part], FC.at[(lead, hp) + part], (rc, c)),
+            7: (A.at[(lead, rcs, 1) + part], FC.at[(lead, 1) + part], (rc, c)),
+            2: (A.at[(lead, rxs, fp) + part], FR.at[(lead, fp) + part], (rx, c)),
+            5: (A.at[(lead, rxs, hp) + part], FR.at[(lead, hp) + part], (rx, c)),
+            4: (A.at[(lead, rxs, 1) + part], FR.at[(lead, 1) + part], (rx, c)),
+            1: (A.at[(lead, 1, fp) + part], FX.at[(lead,) + part], (r, cf)),
+            3: (A.at[(lead, 1, hp) + part], FY.at[(lead,) + part], (r, cp)),
+        }[k]
+        return remote(src, dst, f_send, f_recv, ph, L, q, k, dev)
+
+    def f_begin(ph):
+        @pl.when(has_x)
+        def _():
+            for L, q in chunks(ph):
+                f_copy(ph, 2, L, q).start()
+            f_copy(ph, 5).start()
+            f_copy(ph, 4).start()
+
+        for L, q in chunks(ph):
+            f_copy(ph, 0, L, q).start()
+        f_copy(ph, 6).start()
+        f_copy(ph, 7).start()
+
+    def f_core(ph):
+        for L, q in chunks(ph):
+            part = pl.ds(q * CHUNK, CHUNK)
+            f_copy(ph, 0, L, q).wait_recv()
+            pl.when(has_x)(lambda: f_copy(ph, 2, L, q).wait_recv())
+            A[L, 1, fp, part] += FC[L, fp, part] + FR[L, fp, part]
+            pl.when(has_far)(lambda: f_copy(ph, 1, L, q).start())
+        f_copy(ph, 6).wait_recv()
+        pl.when(has_x)(lambda: f_copy(ph, 5).wait_recv())
+        for L, q in chunks(ph):
+            part = pl.ds(q * CHUNK, CHUNK)
+            A[L, 1, hp, part] += FC[L, hp, part] + FR[L, hp, part]
+
+    def f_across(ph):
+        for L, q in chunks(ph):
+            part = pl.ds(q * CHUNK, CHUNK)
+            pl.when(has_cx)(lambda: f_copy(ph, 1, L, q).wait_recv())
+            A[L, 1, hp, part] += FX[L, part]
+            f_copy(ph, 3, L, q).start()
+        f_copy(ph, 7).wait_recv()
+        pl.when(has_x)(lambda: f_copy(ph, 4).wait_recv())
+        for L, q in chunks(ph):
+            part = pl.ds(q * CHUNK, CHUNK)
+            A[L, 1, 1, part] += FC[L, 1, part] + FR[L, 1, part]
+
+    def f_end(ph, L, q):
         part = pl.ds(q * CHUNK, CHUNK)
-        src, dst, dev = {
-            0: (A.at[L, rcs, fp, part], FC.at[L, fp, part], (rc, c)),
-            6: (A.at[L, rcs, hp, part], FC.at[L, hp, part], (rc, c)),
-            7: (A.at[L, rcs, 1, part], FC.at[L, 1, part], (rc, c)),
-            2: (A.at[L, rxs, fp, part], FR.at[L, fp, part], (rx, c)),
-            5: (A.at[L, rxs, hp, part], FR.at[L, hp, part], (rx, c)),
-            4: (A.at[L, rxs, 1, part], FR.at[L, 1, part], (rx, c)),
-            1: (A.at[L, 1, fp, part], FX.at[L, part], (r, cf)),
-            3: (A.at[L, 1, hp, part], FY.at[L, part], (r, cp)),
-        }[k]
-        return pltpu.make_async_remote_copy(
-            src_ref=src,
-            dst_ref=dst,
-            send_sem=f_send.at[L, k, q],
-            recv_sem=f_recv.at[L, k, q],
-            device_id={"rows": dev[0], "cols": dev[1]},
-            device_id_type=MESH,
-        )
-
-    def f_start(L, k, q):
-        when(f_sends.get(k, always), lambda: f_copy(L, k, q).start())
-
-    def f_wait(L, k, q):
-        when(f_recvs.get(k, always), lambda: f_copy(L, k, q).wait_recv())
-
-    def f_begin(planes, kinds=(0, 2, 6, 5, 7, 4)):
-        for k in kinds:
-            start_all(f_copy, f_sends, planes, k)
-
-    def f_core(planes):
-        for L, q in chunks(planes):
-            part = pl.ds(q * CHUNK, CHUNK)
-            f_wait(L, 0, q)
-            f_wait(L, 2, q)
-            A[L, 1, fp, part] += FC[L, fp, part] + FR[L, fp, part]
-            f_start(L, 1, q)
-        for L, q in chunks(planes):
-            part = pl.ds(q * CHUNK, CHUNK)
-            f_wait(L, 6, q)
-            f_wait(L, 5, q)
-            A[L, 1, hp, part] += FC[L, hp, part] + FR[L, hp, part]
-
-    def f_across(planes):
-        for L, q in chunks(planes):
-            part = pl.ds(q * CHUNK, CHUNK)
-            f_wait(L, 1, q)
-            A[L, 1, hp, part] += FX[L, part]
-            f_start(L, 3, q)
-
-    def f_end(L, q):
-        part = pl.ds(q * CHUNK, CHUNK)
-        for k in (7, 4, 3):
-            f_wait(L, k, q)
-        return A[L, 1, 1, part] + FC[L, 1, part] + FR[L, 1, part] + FY[L, part]
+        f_copy(ph, 3, L, q).wait_recv()
+        return A[L, 1, 1, part] + FY[L, part]
+
+    def drain(copy, sends, ph):
+        for k in range(8):
+            when(sends.get(k, always), lambda: copy(ph, k).wait_send())
 
     local[3].wait()
     local[4].wait()
     greeted = 2 + has_x.astype(jnp.int32) + has_cx.astype(jnp.int32) + has_far.astype(jnp.int32)
     pl.semaphore_wait(barrier, greeted)
-    g_begin((0, 1), (1, 2, 0))
+    for L, q in chunks(0):
+        g_copy(0, 1, L, q).start()
+    g_begin(0)
 
     zero_tile = jnp.zeros((T, T), f32)
 
@@ -318,7 +318,7 @@
         return carry
 
     lax.fori_loop(0, n_pos, roll_probe, 0)
-    light = (2 * ITERS,)
+    light = ITERS
     f_begin(light)
 
     local[1].wait()
@@ -441,36 +441,32 @@
     g_finish(0, lambda: f_core(light))
     f_across(light)
     for it in range(ITERS):
-        planes = (2 * it, 2 * it + 1)
         every(window, 5, it)
-        f_begin(planes)
+        f_begin(it)
         every(after, 2, it)
         if it == 0:
-            for _, q in chunks(light):
-                ill[pl.ds(q * CHUNK, CHUNK)] = f_end(2 * ITERS, q) + 1.0
-        f_core(planes)
-        f_across(planes)
-        for L, q in chunks(planes):
+            for L, q in chunks(light):
+                ill[pl.ds(q * CHUNK, CHUNK)] = f_end(light, L, q) + 1.0
+        f_core(it)
+        if it == ITERS - 1:
+            drain(f_copy, f_sends, light)
+            for done in range(ITERS):
+                drain(g_copy, g_sends, done)
+            for done in range(ITERS - 1):
+                drain(f_copy, f_sends, done)
+        f_across(it)
+        for L, q in chunks(it):
             part = pl.ds(q * CHUNK, CHUNK)
-            new = G[L, 1, 1, part] - f_end(L, q) / ill[part]
+            new = G[L, 1, 1, part] - f_end(it, L, q) / ill[part]
             if it < ITERS - 1:
                 G[L + 2, 1, 1, part] = new
-                g_start(L + 2, 1, q)
+                g_copy(it + 1, 1, L + 2, q).start()
             else:
                 out_ref[L - 2 * it, part] = new
         if it < ITERS - 1:
-            planes = (2 * it + 2, 2 * it + 3)
-            g_begin(planes, (2, 0))
+            g_begin(it + 1)
             g_finish(it + 1)
-
-    for copy, sends, planes in ((g_copy, g_sends, 2 * ITERS), (f_copy, f_sends, 2 * ITERS + 1)):
-        for k in range(8):
-
-            def drain():
-                for L, q in chunks(range(planes)):
-                    copy(L, k, q).wait_send()
-
-            when(sends.get(k, always), drain)
+    drain(f_copy, f_sends, ITERS - 1)
 
 
 def local(n_rows, n_cols, object_field, probe, amplitudes, offsets):
@@ -502,9 +498,9 @@
             pltpu.VMEM((n_pos, 2, T, W), f32),
             pltpu.VMEM((2, W, T), f32),
             pltpu.VMEM((n_pos, 2, T, W), f32),
+            pltpu.SemaphoreType.DMA((ITERS, 8)),
             pltpu.SemaphoreType.DMA((n, 8, T // CHUNK)),
-            pltpu.SemaphoreType.DMA((n, 8, T // CHUNK)),
-            pltpu.SemaphoreType.DMA((n + 1, 8, T // CHUNK)),
+            pltpu.SemaphoreType.DMA((ITERS + 1, 8)),
             pltpu.SemaphoreType.DMA((n + 1, 8, T // CHUNK)),
             pltpu.SemaphoreType.DMA((5,)),
         ],

time: 59.5 us -> 57.9 us (0.973)
  Pallas kernels: 58.7 us -> 57.1 us
    pallas_call x1, Pallas kernels: 58.7 us -> 57.1 us  [local(): pl.pallas_call(functools.partial(kernel, n_rows, n_cols, n_pos), out_shap...]
where the time goes in v3:
time: 57.9 us; the launch traced here: 57.8 us
  Pallas kernels  57.1 us (99%)
  local copies, waits for them, and re-layouts  0.66 us (1%)
    pallas_call x1, Pallas kernels, local(): pl.pallas_call(functools.partial(kernel, n_rows, n_cols, n_pos), out_shap...  57.1 us

profile of v3, /device:TPU:96, one launch (start us, length us, event | category | flops | bytes accessed | tf_op | source)
XLA Modules:
  0.0 57.8 jit_solution(16090842811176656145)
XLA Ops:
  0.0 57.1 %shard_map.55 = f32[2,128,128]{2,1,0:T(8,128)S(1)} custom-call(f32[2,128,128]{2,1,0:T(8,128)} %obj_hbm.1, s32[2,4]{1,0:T(2,128)} %bitcast.5, f32[2,256,256]{2,1,0:T(8,128)} %probe_hbm.1, f32[4,256,256]{2,1,0:T(8,128)} %bitcast.4, bf16[8,256,256]{2,1,0:T(8,128)(2,1)} %constant.2.clone.mats_hbm), custom_call_target="tpu_custom_call" | custom-call | tf_op jit(solution)/shard_map/pallas_call | solution.py:481
  57.1 0.7 %copy.7 = f32[2,128,128]{2,1,0:T(8,128)} copy(f32[2,128,128]{2,1,0:T(8,128)S(1)} %shard_map.55) | data formatting | bytes 262144

commit v4 on v3

--- a/solution.py
+++ b/solution.py
@@ -68,6 +68,30 @@
     hp = cp - c + 1
     fp = 2 - hp
 
+    barrier = pltpu.get_barrier_semaphore()
+
+    def greet(row, col):
+        pl.semaphore_signal(
+            barrier, inc=1, device_id={"rows": row, "cols": col}, device_id_type=MESH
+        )
+
+    @pl.when(has_cx)
+    def _():
+        greet(r, cx)
+
+    @pl.when(has_far)
+    def _():
+        greet(r, cf)
+
+    greet(r, cp)
+
+    @pl.when(has_x)
+    def _():
+        greet(rx, c)
+        greet(rx, cp)
+
+    greet(rc, c)
+
     local = [
         pltpu.make_async_copy(probe_hbm, probe, l_sem.at[0]),
         pltpu.make_async_copy(amp_hbm, amp, l_sem.at[1]),
@@ -78,28 +102,6 @@
     for i in (3, 4, 0, 1, 2):
         local[i].start()
 
-    barrier = pltpu.get_barrier_semaphore()
-
-    def greet(row, col):
-        pl.semaphore_signal(
-            barrier, inc=1, device_id={"rows": row, "cols": col}, device_id_type=MESH
-        )
-
-    greet(rc, c)
-    greet(r, cp)
-
-    @pl.when(has_x)
-    def _():
-        greet(rx, c)
-
-    @pl.when(has_cx)
-    def _():
-        greet(r, cx)
-
-    @pl.when(has_far)
-    def _():
-        greet(r, cf)
-
     always = None
 
     def both(a, b):
@@ -138,7 +140,7 @@
             0: ((1, 1), (2 - rcs, 1), (rc, c)),
             1: ((1, 1), (1, 2 - hp), (r, cp)),
             2: ((1, 1), (2 - rxs, 1), (rx, c)),
-            3: ((1, hp), (2 - rxs, hp), (rx, c)),
+            3: ((1, 1), (2 - rxs, 2 - hp), (rx, cp)),
             4: ((1, hp), (1, fp), (r, cx)),
             5: ((1, fp), (2 - rxs, fp), (rx, c)),
             6: ((1, hp), (2 - rcs, hp), (rc, c)),
@@ -151,14 +153,18 @@
 
     def g_begin(ph):
         g_copy(ph, 0).start()
-        pl.when(has_x)(lambda: g_copy(ph, 2).start())
+
+        @pl.when(has_x)
+        def _():
+            g_copy(ph, 3).start()
+            g_copy(ph, 2).start()
+
 
     def g_finish(ph, meanwhile=None):
         for L, q in chunks(ph):
             g_copy(ph, 1, L, q).wait_recv()
             pl.when(has_cx)(lambda: g_copy(ph, 4, L, q).start())
         g_copy(ph, 6).start()
-        pl.when(has_x)(lambda: g_copy(ph, 3).start())
         if meanwhile is not None:
             meanwhile()
 
@@ -193,7 +199,7 @@
             6: (A.at[(lead, rcs, hp) + part], FC.at[(lead, hp) + part], (rc, c)),
             7: (A.at[(lead, rcs, 1) + part], FC.at[(lead, 1) + part], (rc, c)),
             2: (A.at[(lead, rxs, fp) + part], FR.at[(lead, fp) + part], (rx, c)),
-            5: (A.at[(lead, rxs, hp) + part], FR.at[(lead, hp) + part], (rx, c)),
+            5: (A.at[(lead, rxs, hp) + part], FR.at[(lead, 2 - hp) + part], (rx, cp)),
             4: (A.at[(lead, rxs, 1) + part], FR.at[(lead, 1) + part], (rx, c)),
             1: (A.at[(lead, 1, fp) + part], FX.at[(lead,) + part], (r, cf)),
             3: (A.at[(lead, 1, hp) + part], FY.at[(lead,) + part], (r, cp)),
@@ -206,7 +212,6 @@
             for L, q in chunks(ph):
                 f_copy(ph, 2, L, q).start()
             f_copy(ph, 5).start()
-            f_copy(ph, 4).start()
 
         for L, q in chunks(ph):
             f_copy(ph, 0, L, q).start()
@@ -220,11 +225,11 @@
             pl.when(has_x)(lambda: f_copy(ph, 2, L, q).wait_recv())
             A[L, 1, fp, part] += FC[L, fp, part] + FR[L, fp, part]
             pl.when(has_far)(lambda: f_copy(ph, 1, L, q).start())
+        pl.when(has_x)(lambda: f_copy(ph, 4).start())
         f_copy(ph, 6).wait_recv()
-        pl.when(has_x)(lambda: f_copy(ph, 5).wait_recv())
         for L, q in chunks(ph):
             part = pl.ds(q * CHUNK, CHUNK)
-            A[L, 1, hp, part] += FC[L, hp, part] + FR[L, hp, part]
+            A[L, 1, hp, part] += FC[L, hp, part]
 
     def f_across(ph):
         for L, q in chunks(ph):
@@ -233,10 +238,15 @@
             A[L, 1, hp, part] += FX[L, part]
             f_copy(ph, 3, L, q).start()
         f_copy(ph, 7).wait_recv()
-        pl.when(has_x)(lambda: f_copy(ph, 4).wait_recv())
+
+        @pl.when(has_x)
+        def _():
+            f_copy(ph, 4).wait_recv()
+            f_copy(ph, 5).wait_recv()
+
         for L, q in chunks(ph):
             part = pl.ds(q * CHUNK, CHUNK)
-            A[L, 1, 1, part] += FC[L, 1, part] + FR[L, 1, part]
+            A[L, 1, 1, part] += FC[L, 1, part] + FR[L, 1, part] + FR[L, hp, part]
 
     def f_end(ph, L, q):
         part = pl.ds(q * CHUNK, CHUNK)
@@ -249,7 +259,7 @@
 
     local[3].wait()
     local[4].wait()
-    greeted = 2 + has_x.astype(jnp.int32) + has_cx.astype(jnp.int32) + has_far.astype(jnp.int32)
+    greeted = 2 + 2 * has_x.astype(jnp.int32) + has_cx.astype(jnp.int32) + has_far.astype(jnp.int32)
     pl.semaphore_wait(barrier, greeted)
     for L, q in chunks(0):
         g_copy(0, 1, L, q).start()

time: 57.9 us -> 57 us (0.984)
  Pallas kernels: 57.1 us -> 56.2 us
    pallas_call x1, Pallas kernels: 57.1 us -> 56.2 us  [local(): pl.pallas_call(functools.partial(kernel, n_rows, n_cols, n_pos), out_shap...]
where the time goes in v4:
time: 57 us; the launch traced here: 56.9 us
  Pallas kernels  56.2 us (99%)
  local copies, waits for them, and re-layouts  0.66 us (1%)
    pallas_call x1, Pallas kernels, local(): pl.pallas_call(functools.partial(kernel, n_rows, n_cols, n_pos), out_shap...  56.2 us

profile of v4, /device:TPU:96, one launch (start us, length us, event | category | flops | bytes accessed | tf_op | source)
XLA Modules:
  0.0 56.9 jit_solution(13513785828303130467)
XLA Ops:
  0.0 56.2 %shard_map.55 = f32[2,128,128]{2,1,0:T(8,128)S(1)} custom-call(f32[2,128,128]{2,1,0:T(8,128)} %obj_hbm.1, s32[2,4]{1,0:T(2,128)} %bitcast.5, f32[2,256,256]{2,1,0:T(8,128)} %probe_hbm.1, f32[4,256,256]{2,1,0:T(8,128)} %bitcast.4, bf16[8,256,256]{2,1,0:T(8,128)(2,1)} %constant.2.clone.mats_hbm), custom_call_target="tpu_custom_call" | custom-call | tf_op jit(solution)/shard_map/pallas_call | solution.py:491
  56.2 0.7 %copy.7 = f32[2,128,128]{2,1,0:T(8,128)} copy(f32[2,128,128]{2,1,0:T(8,128)S(1)} %shard_map.55) | data formatting | bytes 262144

commit v5 on v4

--- a/solution.py
+++ b/solution.py
@@ -157,7 +157,6 @@
         @pl.when(has_x)
         def _():
             g_copy(ph, 3).start()
-            g_copy(ph, 2).start()
 
 
     def g_finish(ph, meanwhile=None):
@@ -165,6 +164,7 @@
             g_copy(ph, 1, L, q).wait_recv()
             pl.when(has_cx)(lambda: g_copy(ph, 4, L, q).start())
         g_copy(ph, 6).start()
+        pl.when(has_x)(lambda: g_copy(ph, 2).start())
         if meanwhile is not None:
             meanwhile()
 

time: 57 us -> 56.9 us (level)
  no operation moved by 1% of the time
where the time goes in v5:
time: 56.9 us; the launch traced here: 56.8 us
  Pallas kernels  56.1 us (99%)
  local copies, waits for them, and re-layouts  0.66 us (1%)
    pallas_call x1, Pallas kernels, local(): pl.pallas_call(functools.partial(kernel, n_rows, n_cols, n_pos), out_shap...  56.1 us

profile of v5, /device:TPU:96, one launch (start us, length us, event | category | flops | bytes accessed | tf_op | source)
XLA Modules:
  0.0 56.8 jit_solution(2864442700636376425)
XLA Ops:
  0.0 56.1 %shard_map.55 = f32[2,128,128]{2,1,0:T(8,128)S(1)} custom-call(f32[2,128,128]{2,1,0:T(8,128)} %obj_hbm.1, s32[2,4]{1,0:T(2,128)} %bitcast.5, f32[2,256,256]{2,1,0:T(8,128)} %probe_hbm.1, f32[4,256,256]{2,1,0:T(8,128)} %bitcast.4, bf16[8,256,256]{2,1,0:T(8,128)(2,1)} %constant.2.clone.mats_hbm), custom_call_target="tpu_custom_call" | custom-call | tf_op jit(solution)/shard_map/pallas_call | solution.py:491
  56.1 0.7 %copy.7 = f32[2,128,128]{2,1,0:T(8,128)} copy(f32[2,128,128]{2,1,0:T(8,128)S(1)} %shard_map.55) | data formatting | bytes 262144
